TPU v7x, 32 devices: a whole 2x2x4 slice. The times are simulated.
32 devices in a mesh: blk: 16 (over z, x, core), grp: 2 (over y).
Axes of the slice: x: 2, y: 2, z: 4, core: 2. Of those that a mesh axis runs over, the one named last changes fastest.
Arguments:
- embeddings: bfloat16 [32768, 1024], P(('blk', 'grp')), may hold values from -6 to 6
Outputs:
- tile_max: float32 [32768, 40], P(('blk', 'grp'))
All inputs are finite; a program needn't handle non-finite values.
Results may differ from a plain program's by a relative error of at most 0.0017.
Values may be sent and summed in bfloat16 or wider, within the bound.
A program may use at most 64 MiB of HBM per device.

v0:
```python
import jax
import jax.numpy as jnp
from jax import lax
from jax.sharding import PartitionSpec as P


def from_behind(block, axis, distance):
    devices = range(lax.axis_size(axis))
    route = [((i - distance) % len(devices), i) for i in devices]
    return lax.ppermute(block, axis, route)


def tile_rows(scores):
    count = scores.shape[0]
    return jnp.max(scores.reshape(count, count // 128, 128), axis=-1)


def tile_columns(scores):
    count = scores.shape[0]
    return jnp.transpose(jnp.max(scores.reshape(count // 128, 128, count), axis=1))


def body(embeddings):
    count, width = embeddings.shape
    values = embeddings.astype(jnp.float32)
    unit = (values * lax.rsqrt(jnp.mean(values * values, axis=-1, keepdims=True) + 1e-06)).astype(
        jnp.bfloat16
    )
    scale = 1.0 / width**0.5

    def score(keys):
        return (
            lax.dot_general(
                unit, keys, (((1,), (1,)), ((), ())), preferred_element_type=jnp.float32
            )
            * scale
        )

    upper_one = from_behind(unit, ("blk", "grp"), -1)
    upper_two = from_behind(unit, ("blk", "grp"), -2)
    same = jnp.arange(count)[:, None] == jnp.arange(count)[None, :]
    own_max = tile_rows(jnp.where(same, -jnp.inf, score(unit)))
    score_one = score(upper_one)
    score_two = score(upper_two)
    lower_one = from_behind(tile_columns(score_one), ("blk", "grp"), 1)
    lower_two = from_behind(tile_columns(score_two), ("blk", "grp"), 2)
    return jnp.concatenate(
        [lower_two, lower_one, own_max, tile_rows(score_one), tile_rows(score_two)], axis=1
    )


def solution(mesh):
    return jax.shard_map(
        body,
        mesh=mesh,
        in_specs=(P(("blk", "grp"), None),),
        out_specs=P(("blk", "grp"), None),
        check_vma=False,
    )
```

profile of v0, /device:TPU:0, one launch (start us, length us, event | category | flops | bytes accessed | tf_op | source)
XLA Modules:
  0.0 85.4 jit_solution(11560941311825042218)
XLA Ops:
  0.0 2.1 %fusion = f32[1024]{0:T(1024)S(1)} fusion(bf16[1024,1024]{1,0:T(8,128)(2,1)} %param.1), kind=kLoop, calls=%fused_computation.2 | loop fusion | flops 3144704 | bytes 2101248 | tf_op jit(solution)/shard_map/reduce_sum | solution.py:26
  2.1 2.0 %fusion.1 = bf16[1024,1024]{1,0:T(8,128)(2,1)S(1)} fusion(bf16[1024,1024]{1,0:T(8,128)(2,1)} %param.1, f32[1024]{0:T(1024)S(1)} %add_rsqrt_fusion), kind=kLoop, calls=%fused_computation.3 | loop fusion | flops 3145728 | bytes 4198400 | tf_op jit(solution)/shard_map/convert_element_type | solution.py:26
  4.1 5.5 %collective-permute-start = (bf16[1024,1024]{1,0:T(8,128)(2,1)S(1)}, bf16[1024,1024]{1,0:T(8,128)(2,1)}, u32[]{:S(2)}, u32[]{:S(2)}) collective-permute-start(bf16[1024,1024]{1,0:T(8,128)(2,1)S(1)} %fusion.1), channel_id=1, source_target_pairs={{2,0},{3,1},{4,2},{5,3},{6,4},{7,5},{8,6},{9,7},{10,8},{11,9},{12,... | collective-permute-start | bytes 6291464 | tf_op jit(solution)/shard_map/ppermute | solution.py:10
  9.6 1.6 %collective-permute-start.2 = (bf16[1024,1024]{1,0:T(8,128)(2,1)S(1)}, bf16[1024,1024]{1,0:T(8,128)(2,1)}, u32[]{:S(2)}, u32[]{:S(2)}) collective-permute-start(bf16[1024,1024]{1,0:T(8,128)(2,1)S(1)} %fusion.1), channel_id=1, source_target_pairs={{1,0},{2,1},{3,2},{4,3},{5,4},{6,5},{7,6},{8,7},{9,8},{10,9},{11,1... | collective-permute-start | bytes 6291464 | tf_op jit(solution)/shard_map/ppermute | solution.py:10
  11.2 2.4 %select_bitcast_fusion = f32[128,8,8,128]{3,1,2,0:T(8,128)S(1)} fusion(bf16[1024,1024]{1,0:T(8,128)(2,1)S(1)} %fusion.1), kind=kOutput, calls=%fused_computation.6 | convolution fusion | flops 2150629376 | bytes 6291456 | tf_op jit(solution)/shard_map/dot_general | solution.py:33
  13.6 3.0 %copy.10 = f32[128,8,8,128]{3,2,1,0:T(8,128)} copy(f32[128,8,8,128]{3,1,2,0:T(8,128)S(1)} %select_bitcast_fusion) | data formatting | bytes 8388608
  16.5 3.4 %reduce_max.47 = f32[1024,8]{1,0:T(8,128)S(1)} reduce(f32[1024,8,128]{2,1,0:T(8,128)} %bitcast.20, f32[]{:T(128)} %constant.10.clone.1), dimensions={2}, to_apply=%region_3.4 | reduce | flops 1040384 | bytes 4227076 | tf_op jit(solution)/shard_map/reduce_max | solution.py:15
  19.9 0.2 copy.6
  20.1 13.1 %collective-permute-done = bf16[1024,1024]{1,0:T(8,128)(2,1)} collective-permute-done((bf16[1024,1024]{1,0:T(8,128)(2,1)S(1)}, bf16[1024,1024]{1,0:T(8,128)(2,1)}, u32[]{:S(2)}, u32[]{:S(2)}) %collective-permute-start) | collective-permute-done | bytes 2097184 | tf_op jit(solution)/shard_map/ppermute | solution.py:10
  33.1 4.0 %bitcast_reduce_fusion.1 = (f32[8,1024]{1,0:T(8,128)S(1)}, f32[1024,1024]{1,0:T(8,128)S(1)}) fusion(bf16[1024,1024]{1,0:T(8,128)(2,1)S(1)} %fusion.1, bf16[1024,1024]{1,0:T(8,128)(2,1)} %collective-permute-done), kind=kOutput, calls=%fused_computation.5 | convolution fusion | flops 2149572608 | bytes 8421376 | tf_op jit(solution)/shard_map/dot_general | solution.py:33
  37.1 0.2 collective-permute-start.1
  37.4 18.2 %collective-permute-done.2 = bf16[1024,1024]{1,0:T(8,128)(2,1)} collective-permute-done((bf16[1024,1024]{1,0:T(8,128)(2,1)S(1)}, bf16[1024,1024]{1,0:T(8,128)(2,1)}, u32[]{:S(2)}, u32[]{:S(2)}) %collective-permute-start.2) | collective-permute-done | bytes 2097184 | tf_op jit(solution)/shard_map/ppermute | solution.py:10
  55.6 5.9 %bitcast_reduce_fusion = (f32[8,1024]{1,0:T(8,128)S(1)}, f32[1024,1024]{1,0:T(8,128)}) fusion(bf16[1024,1024]{1,0:T(8,128)(2,1)S(1)} %fusion.1, bf16[1024,1024]{1,0:T(8,128)(2,1)} %collective-permute-done.2), kind=kOutput, calls=%fused_computation.4 | convolution fusion | flops 2149572608 | bytes 8421376 | tf_op jit(solution)/shard_map/dot_general | solution.py:33
  61.5 3.0 %copy.12 = f32[128,8,8,128]{3,2,1,0:T(8,128)} copy(f32[128,8,8,128]{3,1,2,0:T(8,128)S(1)} %bitcast.22) | data formatting | bytes 8388608
  64.5 3.4 %reduce_max.49 = f32[1024,8]{1,0:T(8,128)S(1)} reduce(f32[1024,8,128]{2,1,0:T(8,128)} %bitcast.21, f32[]{:T(128)} %constant.10.clone.1), dimensions={2}, to_apply=%region_5.6 | reduce | flops 1040384 | bytes 4227076 | tf_op jit(solution)/shard_map/reduce_max | solution.py:15
  67.8 0.2 copy.8
  68.0 5.2 %copy.11 = f32[128,8,8,128]{3,2,1,0:T(8,128)} copy(f32[128,8,8,128]{3,1,2,0:T(8,128)} %bitcast.23) | data formatting | bytes 8388608
  73.2 3.4 %reduce_max.48 = f32[1024,8]{1,0:T(8,128)S(1)} reduce(f32[1024,8,128]{2,1,0:T(8,128)} %bitcast.19, f32[]{:T(128)} %constant.10.clone.1), dimensions={2}, to_apply=%region_4.5 | reduce | flops 1040384 | bytes 4227076 | tf_op jit(solution)/shard_map/reduce_max | solution.py:15
  76.6 0.2 copy.7
  76.7 3.6 %collective-permute-start.3 = (f32[1024,8]{0,1:T(8,128)S(1)}, f32[1024,8]{0,1:T(8,128)S(1)}, u32[]{:S(2)}, u32[]{:S(2)}) collective-permute-start(f32[1024,8]{0,1:T(8,128)S(1)} %bitcast.25), channel_id=1, source_target_pairs={{31,0},{0,1},{1,2},{2,3},{3,4},{4,5},{5,6},{6,7},{7,8},{8,9},{9,10... | collective-permute-start | bytes 98312 | tf_op jit(solution)/shard_map/ppermute | solution.py:10
  80.3 0.0 collective-permute-done.1
  80.3 3.8 %collective-permute-done.3 = f32[1024,8]{0,1:T(8,128)S(1)} collective-permute-done((f32[1024,8]{0,1:T(8,128)S(1)}, f32[1024,8]{0,1:T(8,128)S(1)}, u32[]{:S(2)}, u32[]{:S(2)}) %collective-permute-start.3) | collective-permute-done | bytes 32800 | tf_op jit(solution)/shard_map/ppermute | solution.py:10
  84.1 0.0 copy-start
  84.1 0.7 copy-done
  84.8 0.6 constant_dynamic-update-slice_fusion
  (5 shorter events, 0.0 us)
Async XLA Ops:
  4.1 29.1 %collective-permute-start = (bf16[1024,1024]{1,0:T(8,128)(2,1)S(1)}, bf16[1024,1024]{1,0:T(8,128)(2,1)}, u32[]{:S(2)}, u32[]{:S(2)}) collective-permute-start(bf16[1024,1024]{1,0:T(8,128)(2,1)S(1)} %fusion.1), channel_id=1, source_target_pairs={{2,0},{3,1},{4,2},{5,3},{6,4},{7,5},{8,6},{9,7},{10,8},{11,9},{12,... | collective-permute-start | bytes 6291464 | tf_op jit(solution)/shard_map/ppermute | solution.py:10
  9.6 46.0 %collective-permute-start.2 = (bf16[1024,1024]{1,0:T(8,128)(2,1)S(1)}, bf16[1024,1024]{1,0:T(8,128)(2,1)}, u32[]{:S(2)}, u32[]{:S(2)}) collective-permute-start(bf16[1024,1024]{1,0:T(8,128)(2,1)S(1)} %fusion.1), channel_id=1, source_target_pairs={{1,0},{2,1},{3,2},{4,3},{5,4},{6,5},{7,6},{8,7},{9,8},{10,9},{11,1... | collective-permute-start | bytes 6291464 | tf_op jit(solution)/shard_map/ppermute | solution.py:10
  37.1 43.2 %collective-permute-start.1 = (f32[1024,8]{0,1:T(8,128)S(1)}, f32[1024,8]{0,1:T(8,128)S(1)}, u32[]{:S(2)}, u32[]{:S(2)}) collective-permute-start(f32[1024,8]{0,1:T(8,128)S(1)} %bitcast.24), channel_id=1, source_target_pairs={{30,0},{31,1},{0,2},{1,3},{2,4},{3,5},{4,6},{5,7},{6,8},{7,9},{8,1... | collective-permute-start | bytes 98312 | tf_op jit(solution)/shard_map/ppermute | solution.py:10
  76.7 7.3 %collective-permute-start.3 = (f32[1024,8]{0,1:T(8,128)S(1)}, f32[1024,8]{0,1:T(8,128)S(1)}, u32[]{:S(2)}, u32[]{:S(2)}) collective-permute-start(f32[1024,8]{0,1:T(8,128)S(1)} %bitcast.25), channel_id=1, source_target_pairs={{31,0},{0,1},{1,2},{2,3},{3,4},{4,5},{5,6},{6,7},{7,8},{8,9},{9,10... | collective-permute-start | bytes 98312 | tf_op jit(solution)/shard_map/ppermute | solution.py:10
  84.1 0.7 copy-start
where the time goes:
time: 85.8 us; the launch traced here: 85.4 us
  waiting for transfers between devices  35.1 us (41%)
  other arithmetic  14.2 us (17%)
  local copies, waits for them, and re-layouts  12.9 us (15%)
  matrix products  12.2 us (14%)
  starting transfers between devices  10.9 us (13%)
    ppermute x4, waiting for transfers between devices, from_behind(): return lax.ppermute(block, axis, route)  35.1 us
    dot_general x3, matrix products, score(): lax.dot_general(unit, keys, (((1,), (1,)), ((), ())), preferred_element_t...  12.2 us
    unnamed x9, local copies, waits for them, and re-layouts  11.8 us
    ppermute x4, starting transfers between devices, from_behind(): return lax.ppermute(block, axis, route)  10.9 us
    reduce_max x3, other arithmetic, tile_rows(): return jnp.max(scores.reshape(count, count // 128, 128), axis=-1)  10.1 us
    reduce_sum x1, other arithmetic, body(): jnp.mean(values * values, axis=-1, keepdims=True) + 1e-06  2.07 us
    convert_element_type x1, other arithmetic, body(): (values * lax.rsqrt(jnp.mean(values * values, axis=-1, keepdims=True) + 1...  2 us
  transfers between devices with their start and end apart: 4, of which 3 were waited for; matrix products, arithmetic and copies ran while one was open for 40% of the time, Pallas kernels for 0%

commit v1 on v0

v1 whole, which is shorter than its diff:
```python
import functools

import jax
import jax.numpy as jnp
from jax import lax
from jax.experimental import pallas as pl
from jax.experimental.pallas import tpu as pltpu
from jax.sharding import PartitionSpec as P

MESH = pl.DeviceIdType.MESH
CHUNKS = 4
TILE = 128


def unit_rows(raw):
    values = raw.astype(jnp.float32)
    mean = jnp.mean(values * values, axis=-1, keepdims=True)
    return (values * lax.rsqrt(mean + 1e-06)).astype(jnp.bfloat16)


def dot_nt(a, b):
    return lax.dot_general(a, b, (((1,), (1,)), ((), ())), preferred_element_type=jnp.float32)


def kernel(
    names, x_hbm, out_ref, x, u, got, relay, unit_c, res, tiles,
    in_sem, own_send, core_send, far_send, pass_send, relay_send, got_recv, relay_recv, res_send, res_recv,
):
    count, width = x.shape
    rows = count // CHUNKS
    per = rows // TILE
    half = CHUNKS // 2
    scale = 1.0 / width**0.5
    groups = lax.axis_size(names[1])
    total = lax.axis_size(names[0]) * groups
    me = lax.axis_index(names[0]) * groups + lax.axis_index(names[1])
    role = lax.rem(me, 4)
    odd = lax.rem(me // 4, 2)
    is_odd = odd == 1
    even = odd == 0

    def at(offset):
        block = lax.rem(me + offset + total, total)
        return (block // groups, lax.rem(block, groups))

    def pick(a, b, c, d):
        return jnp.where(role == 0, a, jnp.where(role == 1, b, jnp.where(role == 2, c, d)))

    def span(c):
        start = c * rows
        return pl.ds(start if isinstance(c, int) else pl.multiple_of(start, rows), rows)

    def link(src, dst, offset, send, recv):
        return pltpu.make_async_remote_copy(
            src_ref=src, dst_ref=dst, send_sem=send, recv_sem=recv,
            device_id=at(offset), device_id_type=MESH,
        )

    fetch = [
        pltpu.make_async_copy(x_hbm.at[span(c)], x.at[span(c)], in_sem.at[c]) for c in range(CHUNKS)
    ]
    for copy in fetch:
        copy.start()

    barrier = pltpu.get_barrier_semaphore()
    for offset in (-2, -1, 1, 2):
        pl.semaphore_signal(barrier, inc=1, device_id=at(offset), device_id_type=MESH)
    pl.semaphore_wait(barrier, 4)

    def own_copy(c):
        slot = jnp.where(role == 0, 1, 0)
        return link(
            x.at[span(c)], got.at[slot, span(c)], pick(-2, -1, 1, 2),
            own_send.at[c], got_recv.at[slot, c],
        )

    to_core = role >= 2

    def core_copy(c):
        return link(x.at[span(c)], got.at[1, span(c)], -2, core_send.at[c], got_recv.at[1, c])

    to_far = is_odd & ((role == 0) | (role == 3))

    def far_copy(j):
        return link(
            x.at[span(half + j)], relay.at[span(j)], jnp.where(role == 0, 1, -1),
            far_send.at[j], relay_recv.at[j],
        )

    through = is_odd & ((role == 1) | (role == 2))

    def relay_copy(j):
        return link(
            relay.at[span(j)], got.at[2, span(half + j)], jnp.where(role == 1, -2, 2),
            relay_send.at[j], got_recv.at[2, half + j],
        )

    def passes(s, c):
        return jnp.where(
            s == 0,
            (role == 0) | ((role == 1) & even & (c < half)),
            (s == 1) & (role == 2) & even & (c < half),
        )

    def pass_copy(s, c):
        slot = jnp.where(role == 0, 0, 2)
        return link(
            got.at[s, span(c)], got.at[slot, span(c)], pick(2, -1, 1, 1),
            pass_send.at[s, c], got_recv.at[slot, c],
        )

    def offset_of(s):
        return jnp.where(s == 0, pick(1, -2, -1, -1), jnp.where(s == 1, 2, jnp.where(role == 0, -1, 1)))

    def active(s):
        return (s == 0) | ((s == 1) & (role != 3)) | ((s == 2) & even & ((role == 0) | (role == 3)))

    def res_copy(s):
        offset = offset_of(s)
        return link(
            res.at[s], tiles.at[2 - offset], offset, res_send.at[s], res_recv.at[2 - offset],
        )

    for c in range(CHUNKS):
        fetch[c].wait()
        own_copy(c).start()

        @pl.when(to_core)
        def _():
            core_copy(c).start()

        if c >= half:

            @pl.when(to_far)
            def _():
                far_copy(c - half).start()

    def make_unit(c, carry):
        u[span(c), :] = unit_rows(x[span(c), :])
        return carry

    lax.fori_loop(0, CHUNKS, make_unit, 0)

    sub = lax.broadcasted_iota(jnp.int32, (per * CHUNKS, rows), 0)

    def put(place, c, j, scores):
        cols = pl.ds(j * rows, rows)
        held = tiles[place, :, cols]
        for t in range(per):
            top = jnp.max(scores[t * TILE : (t + 1) * TILE], axis=0, keepdims=True) * scale
            held = jnp.where(sub == c * per + t, top, held)
        tiles[place, :, cols] = held

    def own_scores(c, carry):
        mine = u[span(c), :]
        for j in range(CHUNKS):
            scores = dot_nt(mine, u[span(j), :])
            shift = (c - j) * rows
            same = (
                lax.broadcasted_iota(jnp.int32, scores.shape, 0) + shift
                == lax.broadcasted_iota(jnp.int32, scores.shape, 1)
            )
            put(2, c, j, jnp.where(same, -jnp.inf, scores))
        return carry

    lax.fori_loop(0, CHUNKS, own_scores, 0)

    def step(t, carry):
        late = t >= 2 * CHUNKS
        place = t - 2 * CHUNKS
        s = jnp.where(late, 2, lax.rem(t, 2))
        c = jnp.where(late, jnp.where(lax.rem(place, 2) == 0, half, 0) + place // 2, t // 2)

        for j in range(half):

            @pl.when(through & (t == 2 + 2 * j))
            def _():
                link(
                    relay.at[span(j)], relay.at[span(j)], 1, far_send.at[j], relay_recv.at[j]
                ).wait_recv()
                relay_copy(j).start()

        @pl.when(active(s))
        def _():
            link(
                got.at[s, span(c)], got.at[s, span(c)], 1, own_send.at[0], got_recv.at[s, c]
            ).wait_recv()

            @pl.when(passes(s, c))
            def _():
                pass_copy(s, c).start()

            unit_c[...] = unit_rows(got[s, span(c), :])
            theirs = unit_c[...]
            cols = span(c)
            for j in range(CHUNKS):
                scores = dot_nt(u[span(j), :], theirs)
                for i in range(per):
                    top = jnp.max(scores[i * TILE : (i + 1) * TILE], axis=0, keepdims=True) * scale
                    res[s, pl.ds(j * per + i, 1), cols] = top
            offset = offset_of(s)
            for j in range(CHUNKS):
                put(offset + 2, c, j, dot_nt(theirs, u[span(j), :]))

            last = (t == 2 * CHUNKS - 2) | (t == 2 * CHUNKS - 1) | (t == 3 * CHUNKS - 1)

            @pl.when(last)
            def _():
                res_copy(s).start()

        return carry

    lax.fori_loop(0, 3 * CHUNKS, step, 0)

    for c in range(CHUNKS):
        own_copy(c).wait_send()

        @pl.when(to_core)
        def _():
            core_copy(c).wait_send()

        for s in range(2):

            @pl.when(passes(s, c))
            def _():
                pass_copy(s, c).wait_send()

    for j in range(half):

        @pl.when(to_far)
        def _():
            far_copy(j).wait_send()

        @pl.when(through)
        def _():
            relay_copy(j).wait_send()

    for s in range(3):

        @pl.when(active(s))
        def _():
            res_copy(s).wait_send()

    for offset in (-2, -1, 1, 2):
        here = jnp.bool_(False)
        for s in range(3):
            here = here | (active(s) & (offset_of(s) == offset))

        @pl.when(jnp.logical_not(here))
        def _():
            link(
                res.at[0], tiles.at[offset + 2], offset, res_send.at[0], res_recv.at[offset + 2]
            ).wait_recv()

    for i in range(5):
        out_ref[pl.ds(i * per * CHUNKS, per * CHUNKS), :] = tiles[i]


def body(names, embeddings):
    count, width = embeddings.shape
    tiles = count // TILE
    rows = count // CHUNKS
    half = CHUNKS // 2
    bf16 = embeddings.dtype
    dma = pltpu.SemaphoreType.DMA
    wide = pl.pallas_call(
        functools.partial(kernel, names),
        out_shape=jax.ShapeDtypeStruct((5 * tiles, count), jnp.float32),
        in_specs=[pl.BlockSpec(memory_space=pl.ANY)],
        out_specs=pl.BlockSpec(memory_space=pltpu.VMEM),
        scratch_shapes=[
            pltpu.VMEM((count, width), bf16),
            pltpu.VMEM((count, width), bf16),
            pltpu.VMEM((3, count, width), bf16),
            pltpu.VMEM((count // 2, width), bf16),
            pltpu.VMEM((rows, width), bf16),
            pltpu.VMEM((3, tiles, count), jnp.float32),
            pltpu.VMEM((5, tiles, count), jnp.float32),
            dma((CHUNKS,)),
            dma((CHUNKS,)),
            dma((CHUNKS,)),
            dma((half,)),
            dma((2, CHUNKS)),
            dma((half,)),
            dma((3, CHUNKS)),
            dma((half,)),
            dma((3,)),
            dma((5,)),
        ],
        compiler_params=pltpu.CompilerParams(
            collective_id=0, has_side_effects=True, vmem_limit_bytes=60 * 1024 * 1024
        ),
    )(embeddings)
    return jnp.transpose(wide)


def solution(mesh):
    names = ("blk", "grp")
    return jax.shard_map(
        functools.partial(body, names),
        mesh=mesh,
        in_specs=(P(names, None),),
        out_specs=P(names, None),
        check_vma=False,
    )
```

time: 85.8 us -> 52.1 us (0.61)
  Pallas kernels: 0 us -> 50.4 us
  waiting for transfers between devices: 35.1 us -> 0 us
  other arithmetic: 14.2 us -> 0 us
  matrix products: 12.2 us -> 0 us
  local copies, waits for them, and re-layouts: 12.9 us -> 1.59 us
  starting transfers between devices: 10.9 us -> 0 us
    pallas_call x0 -> x1, Pallas kernels: none -> 50.4 us  [body(): pl.pallas_call(functools.partial(kernel, names), out_shape=jax.ShapeDtype...]
    ppermute x4 -> x0, waiting for transfers between devices: 35.1 us -> none  [from_behind(): return lax.ppermute(block, axis, route)]
    dot_general x3 -> x0, matrix products: 12.2 us -> none  [score(): lax.dot_general(unit, keys, (((1,), (1,)), ((), ())), preferred_element_t...]
    ppermute x4 -> x0, starting transfers between devices: 10.9 us -> none  [from_behind(): return lax.ppermute(block, axis, route)]
    unnamed x9 -> x1, local copies, waits for them, and re-layouts: 11.8 us -> 1.59 us
    reduce_max x3 -> x0, other arithmetic: 10.1 us -> none  [tile_rows(): return jnp.max(scores.reshape(count, count // 128, 128), axis=-1)]
    reduce_sum x1 -> x0, other arithmetic: 2.07 us -> none  [body(): jnp.mean(values * values, axis=-1, keepdims=True) + 1e-06]
    convert_element_type x1 -> x0, other arithmetic: 2 us -> none  [body(): (values * lax.rsqrt(jnp.mean(values * values, axis=-1, keepdims=True) + 1...]
  transfers between devices with their start and end apart: 4 -> 0, of which waited for: 3 -> 0; matrix products, arithmetic and copies ran while one was open for 40% -> 0% of each run, Pallas kernels for 0% -> 0%
where the time goes in v1:
time: 52.1 us; the launch traced here: 52 us
  Pallas kernels  50.4 us (97%)
  local copies, waits for them, and re-layouts  1.59 us (3%)
    pallas_call x1, Pallas kernels, body(): pl.pallas_call(functools.partial(kernel, names), out_shape=jax.ShapeDtype...  50.4 us
    unnamed x1, local copies, waits for them, and re-layouts  1.59 us

profile of v1, /device:TPU:0, one launch (start us, length us, event | category | flops | bytes accessed | tf_op | source)
XLA Modules:
  0.0 52.0 jit_solution(14101883567053430824)
XLA Ops:
  0.0 50.4 %shard_map.17 = f32[40,1024]{1,0:T(8,128)} custom-call(bf16[1024,1024]{1,0:T(8,128)(2,1)} %x_hbm.1), custom_call_target="tpu_custom_call" | custom-call | tf_op jit(solution)/shard_map/pallas_call | solution.py:266
  50.4 1.6 %copy.3 = f32[1024,40]{0,1:T(8,128)} copy(f32[1024,40]{0,1:T(8,128)} %bitcast.1) | data formatting | bytes 327680

commit v2 on v1

--- a/solution.py
+++ b/solution.py
@@ -165,15 +165,17 @@
 
     lax.fori_loop(0, CHUNKS, own_scores, 0)
 
+    flip = jnp.where(role == 2, 1, 0)
+
     def step(t, carry):
         late = t >= 2 * CHUNKS
         place = t - 2 * CHUNKS
-        s = jnp.where(late, 2, lax.rem(t, 2))
+        s = jnp.where(late, 2, lax.rem(t + flip, 2))
         c = jnp.where(late, jnp.where(lax.rem(place, 2) == 0, half, 0) + place // 2, t // 2)
 
         for j in range(half):
 
-            @pl.when(through & (t == 2 + 2 * j))
+            @pl.when(through & (t == 1 + 2 * j))
             def _():
                 link(
                     relay.at[span(j)], relay.at[span(j)], 1, far_send.at[j], relay_recv.at[j]
@@ -198,15 +200,15 @@
                 for i in range(per):
                     top = jnp.max(scores[i * TILE : (i + 1) * TILE], axis=0, keepdims=True) * scale
                     res[s, pl.ds(j * per + i, 1), cols] = top
+            last = (t == 2 * CHUNKS - 2) | (t == 2 * CHUNKS - 1) | (t == 3 * CHUNKS - 1)
+
+            @pl.when(last)
+            def _():
+                res_copy(s).start()
+
             offset = offset_of(s)
             for j in range(CHUNKS):
                 put(offset + 2, c, j, dot_nt(theirs, u[span(j), :]))
-
-            last = (t == 2 * CHUNKS - 2) | (t == 2 * CHUNKS - 1) | (t == 3 * CHUNKS - 1)
-
-            @pl.when(last)
-            def _():
-                res_copy(s).start()
 
         return carry
 

time: 52.1 us -> 47.9 us (0.919)
  Pallas kernels: 50.4 us -> 46.1 us
    pallas_call x1, Pallas kernels: 50.4 us -> 46.1 us  [body(): pl.pallas_call(functools.partial(kernel, names), out_shape=jax.ShapeDtype...]
where the time goes in v2:
time: 47.9 us; the launch traced here: 47.7 us
  Pallas kernels  46.1 us (96%)
  local copies, waits for them, and re-layouts  1.59 us (3%)
    pallas_call x1, Pallas kernels, body(): pl.pallas_call(functools.partial(kernel, names), out_shape=jax.ShapeDtype...  46.1 us
    unnamed x1, local copies, waits for them, and re-layouts  1.59 us

profile of v2, /device:TPU:0, one launch (start us, length us, event | category | flops | bytes accessed | tf_op | source)
XLA Modules:
  0.0 47.7 jit_solution(15567293113581161765)
XLA Ops:
  0.0 46.1 %shard_map.17 = f32[40,1024]{1,0:T(8,128)} custom-call(bf16[1024,1024]{1,0:T(8,128)(2,1)} %x_hbm.1), custom_call_target="tpu_custom_call" | custom-call | tf_op jit(solution)/shard_map/pallas_call | solution.py:268
  46.1 1.6 %copy.3 = f32[1024,40]{0,1:T(8,128)} copy(f32[1024,40]{0,1:T(8,128)} %bitcast.1) | data formatting | bytes 327680
